TPU v7x, 32 devices: a whole 2x2x4 slice. The times are simulated.
32 devices in a mesh: blk: 16 (over z, x, core), col: 2 (over y).
Axes of the slice: x: 2, y: 2, z: 4, core: 2. Of those that a mesh axis runs over, the one named last changes fastest.
Arguments:
- blocks: bfloat16 [16, 2, 2048, 2048], P('blk'), may hold values from -0.09375 to 0.09375
- offsets: int32 [16, 2], P('blk'), may hold values from -2 to 2, as said below
- krylov: bfloat16 [16, 64, 32768], P('col', None, 'blk'), may hold values from -6 to 6
- previous: float32 [64, 16, 32768], P(None, 'col', 'blk')
- node_table: float32 [32], replicated, may hold values from -1.5 to 1.5
- node_index: int32 [16], P('col'), may hold values from 0 to 31
- pole_values: float32 [16], P('col'), may hold values from 4 to 16
- scaling: float32 [16], P('col'), may hold values from 0.5 to 2
Outputs:
- new_basis: bfloat16 [16, 64, 32768], P('col', None, 'blk')
- first_coeffs: float32 [64, 64], replicated
- second_coeffs: float32 [64, 64], replicated
- factor: float32 [64, 64], replicated
Inputs may be any that keep to these rules, and one draw needn't show every extreme that they name: `offsets`: each block row's 2 distances are distinct.
All inputs are finite; a program needn't handle non-finite values.
Results may differ from a plain program's by a relative error of at most 0.0012.
Values may be sent and summed in bfloat16 or wider, within the bound.
A program may use at most 128 MiB of HBM per device.

v0:
```python
import functools
import math

import jax
import jax.numpy as jnp
from jax import lax
from jax.experimental import pallas as pl
from jax.experimental.pallas import tpu as pltpu
from jax.sharding import PartitionSpec as P

REACH = 2
WIDTH = 2 * REACH + 1
BF = jnp.bfloat16
F32 = jnp.float32
NT = (((1,), (1,)), ((), ()))
MESH = pl.DeviceIdType.MESH


def split(x):
    high = x.astype(BF)
    return high, (x - high.astype(F32)).astype(BF)


def dot_nt(a, b):
    return lax.dot_general(a, b, NT, preferred_element_type=F32)


def expand_kernel(
    n_blk, n_col, terms, cols, rows, groups,
    offsets, node_index, node_table, pole_values, scaling,
    krylov, blocks, previous,
    wst, pst, sums, last_sum, basis_sum,
    *scratch,
):
    bufs = scratch[:terms]
    (carry, band, prev, image, a_send, a_recv, b_send, b_recv, c_send, c_recv,
     d_send, d_recv, y_send, y_recv, own_sem, band_sem, prev_sem) = scratch[terms:]
    me = lax.axis_index("blk")
    col = lax.axis_index("col")
    core = lax.rem(me, 2)
    chip = lax.div(me, 2)
    par = lax.rem(chip, 2)
    n_chip = n_blk // 2
    n_prev = previous.shape[0]
    partner = (chip + 1 - 2 * par) * 2 + core
    ahead = lax.rem(chip + 2 - 4 * par + n_chip, n_chip) * 2 + core
    behind = lax.rem(chip - 2 + 4 * par + n_chip, n_chip) * 2 + core
    sibling = chip * 2 + 1 - core

    def remote(src, dst, send, recv, blk, colpos=None):
        return pltpu.make_async_remote_copy(
            src_ref=src, dst_ref=dst, send_sem=send, recv_sem=recv,
            device_id=(blk, col if colpos is None else colpos), device_id_type=MESH)

    own = [pltpu.make_async_copy(krylov.at[k], bufs[k].at[REACH], own_sem.at[k]) for k in range(terms)]
    band_copy = [pltpu.make_async_copy(blocks.at[0, c], band.at[c], band_sem.at[c]) for c in range(band.shape[0])]
    prev_copy = pltpu.make_async_copy(previous, prev, prev_sem)
    prev_copy.start()

    barrier = pltpu.get_barrier_semaphore()
    for blk in (partner, ahead, behind, sibling):
        pl.semaphore_signal(barrier, inc=1, device_id=(blk, col), device_id_type=MESH)
    if n_col > 1:
        for shift in (1, n_col - 1):
            pl.semaphore_signal(barrier, inc=1, device_id=(me, lax.rem(col + shift, n_col)), device_id_type=MESH)
    pl.semaphore_wait(barrier, 4 + (2 if n_col > 1 else 0))

    a_copy = [remote(krylov.at[k], bufs[k].at[4 * par], a_send.at[k], a_recv.at[k], partner) for k in range(terms)]
    c_copy = [remote(krylov.at[k], bufs[k].at[1 + 2 * core], c_send.at[k], c_recv.at[k], sibling) for k in range(terms)]
    b_copy = [remote(bufs[k].at[4 - 4 * par], bufs[k].at[4 * par], b_send.at[k], b_recv.at[k], ahead) for k in range(terms)]
    d_copy = [remote(bufs[k].at[4 - 4 * core], bufs[k].at[3 - 2 * core], d_send.at[k], d_recv.at[k], sibling) for k in range(terms)]
    y_copy = remote(krylov.at[terms - 1], carry, y_send, y_recv, me, lax.rem(col + 1, n_col))

    for k in range(terms):
        a_copy[k].start()
    for k in range(terms):
        c_copy[k].start()
    if n_col > 1:
        @pl.when(col < n_col - 1)
        def _():
            y_copy.start()
    for k in range(terms):
        own[k].start()
    for copy in band_copy:
        copy.start()

    @pl.when(col == 0)
    def _():
        carry[...] = jnp.zeros_like(carry)

    lane = 256

    def arrange(t):
        if t == 0:
            prev_copy.wait()
        p_at = t * 16

        def step(i, _):
            at = pl.ds(pl.multiple_of(i * lane, lane), lane)
            high, low = split(jnp.swapaxes(prev[p_at:p_at + 16, :, at], 0, 1))
            pst[:, p_at:p_at + 16, at] = high
            pst[:, n_prev + p_at:n_prev + p_at + 16, at] = low
            return 0
        lax.fori_loop(0, rows // lane, step, 0)

    def basis_term(t):
        part = dot_nt(pst[t], pst[t, :n_prev])
        if t == 0:
            basis_sum[...] = part
        else:
            basis_sum[...] += part

    tile = 256
    n_coupling = band.shape[0]

    def ready(group):
        for t in group:
            c_copy[t].wait_recv()
            d_copy[t].wait_recv()
            own[t].wait()
        if group[0] == 0:
            for copy in band_copy:
                copy.wait()

    def image_part(group, start, count):
        picks = [
            jnp.concatenate([bufs[t][offsets[0, c] + REACH] for t in group], axis=0)
            for c in range(n_coupling)
        ]

        def step(i, _):
            at = pl.ds(pl.multiple_of(i * tile, tile), tile)
            total = dot_nt(picks[0], band[0, at, :])
            for c in range(1, n_coupling):
                total = total + dot_nt(picks[c], band[c, at, :])
            image[group[0] * cols:(group[-1] + 1) * cols, at] = total
            return 0
        lax.fori_loop(start, start + count, step, 0)

    def finish(group):
        for t in group:
            shift = jnp.full((8, 128), node_table[node_index[t]], F32)
            weight = jnp.full((8, 128), scaling[t], F32) / (
                1.0 - shift / jnp.full((8, 128), pole_values[t], F32))
            before = carry if t == 0 else bufs[t - 1].at[REACH]
            if t == 0 and n_col > 1:
                @pl.when(col > 0)
                def _():
                    y_copy.wait_recv()
            work = (
                image[t * cols:(t + 1) * cols, :]
                - shift[:1, :1] * bufs[t][REACH].astype(F32)
                + weight[:1, :1] * before[...].astype(F32)
            )
            high, low = split(work)
            wst[t, :cols] = high
            wst[t, cols:] = low
            top = dot_nt(pst[t], high)
            self_part = dot_nt(wst[t], high)
            extra = dot_nt(pst[t, :n_prev], low)
            if t == 0:
                sums[:2 * n_prev] = top
                sums[2 * n_prev:] = self_part
                last_sum[...] = extra
            else:
                sums[:2 * n_prev] += top
                sums[2 * n_prev:] += self_part
                last_sum[...] += extra

    n_tiles = rows // tile
    plan = {}
    for j in range(n_prev // 16):
        plan.setdefault(j // 2, []).append(functools.partial(arrange, j))
    for t in range(terms):
        plan.setdefault(-(-n_prev // 32) + t // 3, []).append(functools.partial(basis_term, t))
    first = groups[0]
    begin = min(terms - 1, first[-1] + 2)
    plan.setdefault(begin, []).append(functools.partial(ready, first))
    left = terms - begin
    chunk = -(-n_tiles // left)
    for j in range(left):
        count = min(chunk, n_tiles - j * chunk)
        if count > 0:
            plan.setdefault(begin + j, []).append(functools.partial(image_part, first, j * chunk, count))

    for k in range(terms + 1):
        if k < terms:
            a_copy[k].wait_recv()
            b_copy[k].start()

            @pl.when(par == core)
            def _():
                d_copy[k].start()
        if k > 0:
            b_copy[k - 1].wait_recv()

            @pl.when(par != core)
            def _():
                d_copy[k - 1].start()
        for item in plan.get(k, ()):
            item()
    finish(first)
    for group in groups[1:]:
        ready(group)
        image_part(group, 0, n_tiles)
        finish(group)
    for k in range(terms):
        a_copy[k].wait_send()
        b_copy[k].wait_send()
        c_copy[k].wait_send()
        d_copy[k].wait_send()
    if n_col > 1:
        @pl.when(col < n_col - 1)
        def _():
            y_copy.wait_send()


def expand(n_blk, n_col, blocks, offsets, krylov, previous, node_table, node_index, pole_values, scaling):
    terms, cols, rows = krylov.shape
    n_prev = previous.shape[0]
    groups = (tuple(range(terms // 2)), tuple(range(terms // 2, 3 * terms // 4)), tuple(range(3 * terms // 4, terms)))
    smem = pl.BlockSpec(memory_space=pltpu.SMEM)
    hbm = pl.BlockSpec(memory_space=pl.ANY)
    vmem = pl.BlockSpec(memory_space=pltpu.VMEM)
    dma = pltpu.SemaphoreType.DMA
    return pl.pallas_call(
        functools.partial(expand_kernel, n_blk, n_col, terms, cols, rows, groups),
        out_shape=(
            jax.ShapeDtypeStruct((terms, 2 * cols, rows), BF),
            jax.ShapeDtypeStruct((terms, 2 * n_prev, rows), BF),
            jax.ShapeDtypeStruct((2 * n_prev + 2 * cols, cols), F32),
            jax.ShapeDtypeStruct((n_prev, cols), F32),
            jax.ShapeDtypeStruct((2 * n_prev, n_prev), F32),
        ),
        in_specs=[smem] * 5 + [hbm] * 3,
        out_specs=(vmem,) * 5,
        scratch_shapes=[pltpu.VMEM((WIDTH, cols, rows), BF)] * terms + [
            pltpu.VMEM((cols, rows), BF),
            pltpu.VMEM(blocks.shape[1:], BF),
            pltpu.VMEM(previous.shape, F32),
            pltpu.VMEM((terms * cols, rows), F32),
        ] + [dma((terms,))] * 8 + [dma, dma, dma((terms,)), dma((blocks.shape[1],)), dma],
        compiler_params=pltpu.CompilerParams(
            collective_id=0, has_side_effects=True, vmem_limit_bytes=60 * 1024 * 1024),
    )(offsets, node_index, node_table, pole_values, scaling,
      krylov, blocks, previous)


def final_kernel(inverse, mix, wst, pst, out):
    fh, fl = split(inverse[...])
    dh, dl = split(mix[...])
    half_w, half_p = fl.shape[1], dl.shape[1]
    total = jnp.dot(jnp.concatenate([fh, fh], 1), wst[0], preferred_element_type=F32)
    total += jnp.dot(jnp.concatenate([dh, dh], 1), pst[0], preferred_element_type=F32)
    total += jnp.dot(fl, wst[0, :half_w], preferred_element_type=F32)
    total += jnp.dot(dl, pst[0, :half_p], preferred_element_type=F32)
    out[0] = total.astype(BF)


def final(factor_inverse, mix, wst, pst):
    terms, _, rows = wst.shape
    cols = factor_inverse.shape[0]
    whole = pl.BlockSpec(memory_space=pltpu.VMEM)
    per_term = lambda a: pl.BlockSpec((1,) + a.shape[1:], lambda t: (t, 0, 0))
    return pl.pallas_call(
        final_kernel,
        grid=(terms,),
        out_shape=jax.ShapeDtypeStruct((terms, cols, rows), BF),
        in_specs=[whole] * 2 + [per_term(wst), per_term(pst)],
        out_specs=pl.BlockSpec((1, cols, rows), lambda t: (t, 0, 0)),
    )(factor_inverse, mix, wst, pst)


exact_mode = lax.Precision.HIGHEST


def exact(a, b):
    return jnp.dot(a, b, precision=exact_mode)


def body(n_blk, n_col, blocks, offsets, krylov, previous, node_table, node_index, pole_values, scaling):
    terms, cols, rows = krylov.shape
    n_prev = previous.shape[0]
    wst, pst, sums, last, basis = expand(
        n_blk, n_col, blocks, offsets, krylov, previous, node_table, node_index, pole_values, scaling)
    total_size = rows * n_blk * terms * n_col
    inverse_size = 1.0 / total_size
    root_size = math.sqrt(total_size)
    local_cross = (sums[:n_prev] + sums[n_prev:2 * n_prev] + last) * inverse_size
    low = sums[2 * n_prev + cols:]
    local_self = (sums[2 * n_prev:2 * n_prev + cols] + low + low.T) * inverse_size
    low = basis[n_prev:]
    local_basis = (basis[:n_prev] + low + low.T) * inverse_size
    cross, basis_gram, self_gram = lax.psum((local_cross, local_basis, local_self), ("blk", "col"))
    coeff_two = cross - exact(basis_gram, cross)
    combined = cross + coeff_two
    mixed = exact(combined.T, cross)
    gram = self_gram - mixed - mixed.T + exact(combined.T, exact(basis_gram, combined))
    factor = jnp.linalg.cholesky(gram)
    identity = jnp.eye(cols, dtype=F32)
    inverse_factor = jax.scipy.linalg.solve_triangular(factor, identity, lower=True)
    new_basis = final(inverse_factor, -exact(inverse_factor, combined.T), wst, pst)
    return (new_basis, cross * root_size, coeff_two * root_size, factor)


def solution(mesh):
    in_specs = (
        P("blk", None, None, None),
        P("blk", None),
        P("col", None, "blk"),
        P(None, "col", "blk"),
        P(),
        P("col"),
        P("col"),
        P("col"),
    )
    out_specs = (P("col", None, "blk"), P(), P(), P())
    call = functools.partial(body, mesh.shape["blk"], mesh.shape["col"])
    return jax.shard_map(call, mesh=mesh, in_specs=in_specs, out_specs=out_specs, check_vma=False)
```

profile of v0, /device:TPU:0, one launch (start us, length us, event | category | flops | bytes accessed | tf_op | source)
XLA Modules:
  0.0 149.9 jit_solution(7675983899719859967)
XLA Ops:
  0.6 80.7 %shard_map.111 = (bf16[8,128,2048]{2,1,0:T(8,128)(2,1)}, bf16[8,128,2048]{2,1,0:T(8,128)(2,1)}, f32[256,64]{1,0:T(8,128)}, f32[64,64]{1,0:T(8,128)}, f32[128,64]{1,0:T(8,128)}) custom-call(s32[1,2]{1,0:T(1,128)} %offsets.1, s32[8]{0:T(128)} %node_index.1, f32[32]{0:T(128)} %node_table.1, f32[8]{0:T(128)} %pole_values.1, f32[8]{0:T(128)} %scaling.1, ...), custom_call_target="tpu_custom_call" | custom-call | tf_op jit(solution)/shard_map/pallas_call | solution.py:226
  81.3 0.8 copy.15
  82.1 0.8 slice_add_fusion.1
  82.9 0.1 copy.16
  83.0 0.8 slice_add_fusion.2
  83.8 0.1 copy.12
  83.9 0.8 fusion.5
  84.7 1.0 copy.13
  85.7 0.1 fusion.1
  85.7 39.4 %all-reduce = (f32[64,64]{0,1:T(8,128)S(1)}, f32[64,64]{0,1:T(8,128)S(1)}, f32[64,64]{0,1:T(8,128)S(1)}) all-reduce(f32[64,64]{0,1:T(8,128)S(1)} %fusion.1, f32[64,64]{0,1:T(8,128)S(1)} %get-tuple-element.27, f32[64,64]{0,1:T(8,128)S(1)} %get-tuple-element.28), channel_id=1, replica_groups=mesh['blk'=16,'col'=2] {'blk','col'}, use_global_device_ids=true, to_apply=%region_1.0 | all-reduce | flops 12288 | bytes 98304 | tf_op jit(solution)/shard_map/psum | solution.py:294
  125.2 0.2 broadcast_multiply_fusion
  125.3 0.2 fusion.7
  125.5 0.2 fusion.8
  125.8 0.7 copy.22
  126.5 0.7 copy.21
  127.2 0.1 copy.18
  127.2 0.2 convolution_add_fusion
  127.5 0.1 copy.20
  127.6 5.8 %cholesky.17 = f32[64,64]{1,0:T(8,128)S(1)} custom-call(f32[64,64]{1,0:T(8,128)S(1)} %fusion.4), custom_call_target="Cholesky" | custom-call | tf_op jit(solution)/shard_map/jit(cholesky)/cholesky | solution.py:299
  133.5 0.6 compare_reduce_fusion
  134.1 1.3 select_bitcast_fusion
  135.4 4.9 %custom-call.7 = f32[1,64,64]{1,2,0:T(8,128)S(1)} custom-call(f32[1,64,64]{2,1,0:T(8,128)S(1)} %get-tuple-element.21), custom_call_target="InvertDiagBlocksLowerTriangular" | custom-call | tf_op jit(solution)/shard_map/jit(_solve_triangular)/triangular_solve | solution.py:301
  140.3 0.2 fusion.2.inverse
  140.5 0.0 copy-start
  140.5 0.8 convolution_negate_fusion.mix
  141.3 0.0 copy-done
  141.3 8.6 %shard_map.112 = bf16[8,64,2048]{2,1,0:T(8,128)(2,1)} custom-call(f32[64,64]{1,0:T(8,128)} %copy-done, f32[64,64]{1,0:T(8,128)} %convolution_negate_fusion.mix, bf16[8,128,2048]{2,1,0:T(8,128)(2,1)} %get-tuple-element.12.wst, bf16[8,128,2048]{2,1,0:T(8,128)(2,1)} %get-tuple-element.13.pst), custom_call_target="tpu_custom_call" | custom-call | tf_op jit(solution)/shard_map/pallas_call | solution.py:265
  (2 shorter events, 0.0 us)
Async XLA Ops:
  140.5 0.8 copy-start
where the time goes:
time: 151 us; the launch traced here: 150 us
  Pallas kernels  89.3 us (59%)
  blocking collectives  39.4 us (26%)
  other arithmetic  15.1 us (10%)
  local copies, waits for them, and re-layouts  3.51 us (2%)
  matrix products  1.84 us (1%)
    pallas_call x1, Pallas kernels, expand(): pl.pallas_call(functools.partial(expand_kernel, n_blk, n_col, terms, cols...  80.7 us
    psum x1, blocking collectives, body(): lax.psum((local_cross, local_basis, local_self), ('blk', 'col'))  39.4 us
    pallas_call x1, Pallas kernels, final(): pl.pallas_call(final_kernel, grid=(terms,), out_shape=jax.ShapeDtypeStruc...  8.6 us
    another operation x3, other arithmetic, body(): factor = jnp.linalg.cholesky(gram)  6.52 us
    another operation x2, other arithmetic, body(): jax.scipy.linalg.solve_triangular(factor, identity, lower=True)  6.16 us

commit v1 on v0

--- a/solution.py
+++ b/solution.py
@@ -29,12 +29,14 @@
     n_blk, n_col, terms, cols, rows, groups,
     offsets, node_index, node_table, pole_values, scaling,
     krylov, blocks, previous,
-    wst, pst, sums, last_sum, basis_sum,
+    w_out, p_out, reduced,
     *scratch,
 ):
     bufs = scratch[:terms]
     (carry, band, prev, image, a_send, a_recv, b_send, b_recv, c_send, c_recv,
-     d_send, d_recv, y_send, y_recv, own_sem, band_sem, prev_sem) = scratch[terms:]
+     d_send, d_recv, y_send, y_recv, own_sem, band_sem, prev_sem,
+     wst, pst, sums, last_sum, basis_sum, part, rs_buf, z_buf, ag_buf,
+     w_sem, p_sem, rs_send, rs_recv, z_send, z_recv, ag_send, ag_recv) = scratch[terms:]
     me = lax.axis_index("blk")
     col = lax.axis_index("col")
     core = lax.rem(me, 2)
@@ -44,7 +46,6 @@
     n_prev = previous.shape[0]
     partner = (chip + 1 - 2 * par) * 2 + core
     ahead = lax.rem(chip + 2 - 4 * par + n_chip, n_chip) * 2 + core
-    behind = lax.rem(chip - 2 + 4 * par + n_chip, n_chip) * 2 + core
     sibling = chip * 2 + 1 - core
 
     def remote(src, dst, send, recv, blk, colpos=None):
@@ -57,13 +58,25 @@
     prev_copy = pltpu.make_async_copy(previous, prev, prev_sem)
     prev_copy.start()
 
+    team, depth = part.shape[0], z_buf.shape[0]
+    place = lax.rem(me, 4)
+    layer = lax.div(me, 4)
+    pos = place * n_col + col
+
+    def member(j):
+        other = lax.rem(pos + j, team)
+        return other, layer * 4 + lax.div(other, n_col), lax.rem(other, n_col)
+
+    def peer(j):
+        return lax.rem(layer + j, depth) * 4 + place
+
     barrier = pltpu.get_barrier_semaphore()
-    for blk in (partner, ahead, behind, sibling):
-        pl.semaphore_signal(barrier, inc=1, device_id=(blk, col), device_id_type=MESH)
-    if n_col > 1:
-        for shift in (1, n_col - 1):
-            pl.semaphore_signal(barrier, inc=1, device_id=(me, lax.rem(col + shift, n_col)), device_id_type=MESH)
-    pl.semaphore_wait(barrier, 4 + (2 if n_col > 1 else 0))
+    for j in range(1, team):
+        _, blk, at_col = member(j)
+        pl.semaphore_signal(barrier, inc=1, device_id=(blk, at_col), device_id_type=MESH)
+    for j in range(1, depth):
+        pl.semaphore_signal(barrier, inc=1, device_id=(peer(j), col), device_id_type=MESH)
+    pl.semaphore_wait(barrier, team + depth - 2)
 
     a_copy = [remote(krylov.at[k], bufs[k].at[4 * par], a_send.at[k], a_recv.at[k], partner) for k in range(terms)]
     c_copy = [remote(krylov.at[k], bufs[k].at[1 + 2 * core], c_send.at[k], c_recv.at[k], sibling) for k in range(terms)]
@@ -88,6 +101,8 @@
     def _():
         carry[...] = jnp.zeros_like(carry)
 
+    w_copy = [pltpu.make_async_copy(wst.at[t], w_out.at[t], w_sem.at[t]) for t in range(terms)]
+    p_copy = pltpu.make_async_copy(pst, p_out, p_sem)
     lane = 256
 
     def arrange(t):
@@ -102,6 +117,8 @@
             pst[:, n_prev + p_at:n_prev + p_at + 16, at] = low
             return 0
         lax.fori_loop(0, rows // lane, step, 0)
+        if p_at + 16 == n_prev:
+            p_copy.start()
 
     def basis_term(t):
         part = dot_nt(pst[t], pst[t, :n_prev])
@@ -155,6 +172,7 @@
             high, low = split(work)
             wst[t, :cols] = high
             wst[t, cols:] = low
+            w_copy[t].start()
             top = dot_nt(pst[t], high)
             self_part = dot_nt(wst[t], high)
             extra = dot_nt(pst[t, :n_prev], low)
@@ -204,15 +222,57 @@
         ready(group)
         image_part(group, 0, n_tiles)
         finish(group)
+    low = sums[2 * n_prev + cols:]
+    head = jnp.concatenate([
+        sums[:n_prev] + sums[n_prev:2 * n_prev] + last_sum[...],
+        sums[2 * n_prev:2 * n_prev + cols] + low + low.T,
+    ], axis=1)
+    low = basis_sum[n_prev:]
+    basis = basis_sum[:n_prev] + low + low.T
+    full = jnp.concatenate([head, jnp.concatenate([basis, jnp.zeros_like(basis)], axis=1)], axis=0)
+    part[...] = full.reshape(part.shape)
+    copies = []
+    for j in range(1, team):
+        other, blk, at_col = member(j)
+        copies.append(remote(part.at[other], rs_buf.at[j - 1], rs_send.at[j - 1], rs_recv.at[j - 1], blk, at_col))
+        copies[-1].start()
+    total = part[pos]
+    for j, copy in enumerate(copies):
+        copy.wait_recv()
+        total = total + rs_buf[j]
+    z_buf[layer] = total
+    z_copies = [
+        remote(z_buf.at[layer], z_buf.at[layer], z_send.at[j - 1], z_recv.at[j - 1], peer(j))
+        for j in range(1, depth)]
+    for copy in z_copies:
+        copy.start()
+    for copy in z_copies:
+        copy.wait_recv()
+    total = z_buf[0]
+    for j in range(1, depth):
+        total = total + z_buf[j]
+    ag_buf[pos] = total
+    ag_copies = []
+    for j in range(1, team):
+        _, blk, at_col = member(j)
+        ag_copies.append(remote(ag_buf.at[pos], ag_buf.at[pos], ag_send.at[j - 1], ag_recv.at[j - 1], blk, at_col))
+        ag_copies[-1].start()
     for k in range(terms):
         a_copy[k].wait_send()
         b_copy[k].wait_send()
         c_copy[k].wait_send()
         d_copy[k].wait_send()
+        w_copy[k].wait()
+    p_copy.wait()
     if n_col > 1:
         @pl.when(col < n_col - 1)
         def _():
             y_copy.wait_send()
+    for copy in ag_copies:
+        copy.wait_recv()
+    reduced[...] = ag_buf[...].reshape(reduced.shape)
+    for copy in copies + z_copies + ag_copies:
+        copy.wait_send()
 
 
 def expand(n_blk, n_col, blocks, offsets, krylov, previous, node_table, node_index, pole_values, scaling):
@@ -223,84 +283,126 @@
     hbm = pl.BlockSpec(memory_space=pl.ANY)
     vmem = pl.BlockSpec(memory_space=pltpu.VMEM)
     dma = pltpu.SemaphoreType.DMA
+    team, depth = 4 * n_col, n_blk // 4
+    height = cols + n_prev
+    piece = (height // team, 2 * cols)
     return pl.pallas_call(
         functools.partial(expand_kernel, n_blk, n_col, terms, cols, rows, groups),
         out_shape=(
             jax.ShapeDtypeStruct((terms, 2 * cols, rows), BF),
             jax.ShapeDtypeStruct((terms, 2 * n_prev, rows), BF),
-            jax.ShapeDtypeStruct((2 * n_prev + 2 * cols, cols), F32),
-            jax.ShapeDtypeStruct((n_prev, cols), F32),
-            jax.ShapeDtypeStruct((2 * n_prev, n_prev), F32),
+            jax.ShapeDtypeStruct((height, 2 * cols), F32),
         ),
         in_specs=[smem] * 5 + [hbm] * 3,
-        out_specs=(vmem,) * 5,
+        out_specs=(hbm, hbm, vmem),
         scratch_shapes=[pltpu.VMEM((WIDTH, cols, rows), BF)] * terms + [
             pltpu.VMEM((cols, rows), BF),
             pltpu.VMEM(blocks.shape[1:], BF),
             pltpu.VMEM(previous.shape, F32),
             pltpu.VMEM((terms * cols, rows), F32),
-        ] + [dma((terms,))] * 8 + [dma, dma, dma((terms,)), dma((blocks.shape[1],)), dma],
+        ] + [dma((terms,))] * 8 + [dma, dma, dma((terms,)), dma((blocks.shape[1],)), dma] + [
+            pltpu.VMEM((terms, 2 * cols, rows), BF),
+            pltpu.VMEM((terms, 2 * n_prev, rows), BF),
+            pltpu.VMEM((2 * n_prev + 2 * cols, cols), F32),
+            pltpu.VMEM((n_prev, cols), F32),
+            pltpu.VMEM((2 * n_prev, n_prev), F32),
+            pltpu.VMEM((team,) + piece, F32),
+            pltpu.VMEM((team - 1,) + piece, F32),
+            pltpu.VMEM((depth,) + piece, F32),
+            pltpu.VMEM((team,) + piece, F32),
+            dma((terms,)), dma,
+            dma((team - 1,)), dma((team - 1,)),
+            dma((depth - 1,)), dma((depth - 1,)),
+            dma((team - 1,)), dma((team - 1,)),
+        ],
         compiler_params=pltpu.CompilerParams(
             collective_id=0, has_side_effects=True, vmem_limit_bytes=60 * 1024 * 1024),
     )(offsets, node_index, node_table, pole_values, scaling,
       krylov, blocks, previous)
 
 
-def final_kernel(inverse, mix, wst, pst, out):
-    fh, fl = split(inverse[...])
-    dh, dl = split(mix[...])
-    half_w, half_p = fl.shape[1], dl.shape[1]
-    total = jnp.dot(jnp.concatenate([fh, fh], 1), wst[0], preferred_element_type=F32)
-    total += jnp.dot(jnp.concatenate([dh, dh], 1), pst[0], preferred_element_type=F32)
-    total += jnp.dot(fl, wst[0, :half_w], preferred_element_type=F32)
-    total += jnp.dot(dl, pst[0, :half_p], preferred_element_type=F32)
-    out[0] = total.astype(BF)
-
-
-def final(factor_inverse, mix, wst, pst):
+def exact(a, b):
+    return jnp.dot(a, b, precision=lax.Precision.HIGHEST, preferred_element_type=F32)
+
+
+def final_kernel(total_size, reduced, w_in, p_in, out, first, second, factor, stack, result, in_sem, out_sem):
+    terms, depth, rows = stack.shape
+    cols = first.shape[1]
+    n_prev = first.shape[0]
+    w_copy = [pltpu.make_async_copy(w_in.at[t], stack.at[t, pl.ds(0, 2 * cols)], in_sem.at[0, t]) for t in range(terms)]
+    p_copy = [pltpu.make_async_copy(p_in.at[t], stack.at[t, pl.ds(2 * cols, 2 * n_prev)], in_sem.at[1, t]) for t in range(terms)]
+    for t in range(terms):
+        w_copy[t].start()
+        p_copy[t].start()
+    inverse_size = 1.0 / total_size
+    root_size = math.sqrt(total_size)
+    cross = reduced[:n_prev, :cols] * inverse_size
+    self_gram = reduced[:n_prev, cols:] * inverse_size
+    basis_gram = reduced[n_prev:, :n_prev] * inverse_size
+    coeff_two = cross - exact(basis_gram, cross)
+    combined = cross + coeff_two
+    turned = combined.T
+    mixed = exact(turned, cross)
+    gram = self_gram - mixed - mixed.T + exact(turned, exact(basis_gram, combined))
+    first[...] = cross * root_size
+    second[...] = coeff_two * root_size
+    row = lax.broadcasted_iota(jnp.int32, (cols, cols), 0)
+    lane = lax.broadcasted_iota(jnp.int32, (cols, cols), 1)
+    both = jnp.concatenate([gram, jnp.where(row == lane, 1.0, 0.0)], axis=1)
+    below = lax.broadcasted_iota(jnp.int32, (cols, 1), 0)
+    for k in range(cols - 1):
+        ratio = jnp.where(below > k, both[:, k:k + 1] * (1.0 / both[k:k + 1, k:k + 1]), 0.0)
+        both = both - ratio * both[k:k + 1, :]
+    left, right = both[:, :cols], both[:, cols:]
+    pivots = jnp.sum(jnp.where(row == lane, left, 0.0), axis=1, keepdims=True)
+    scale = 1.0 / jnp.sqrt(pivots)
+    factor[...] = jnp.where(lane >= row, left * scale, 0.0).T
+    inverse = jnp.where(lane <= row, right * scale, 0.0)
+    mix = -exact(inverse, turned)
+    fh, fl = split(inverse)
+    dh, dl = split(mix)
+    zero_f, zero_d = jnp.zeros_like(fl), jnp.zeros_like(dl)
+    weights = jnp.concatenate([
+        jnp.concatenate([fh, fh, dh, dh], axis=1),
+        jnp.concatenate([fl, zero_f, dl, zero_d], axis=1),
+    ], axis=0)
+    out_copy = [pltpu.make_async_copy(result.at[t], out.at[t], out_sem.at[t]) for t in range(terms)]
+    for t in range(terms):
+        w_copy[t].wait()
+        p_copy[t].wait()
+        both = jnp.dot(weights, stack[t], preferred_element_type=F32)
+        result[t] = (both[:cols] + both[cols:]).astype(BF)
+        out_copy[t].start()
+    for t in range(terms):
+        out_copy[t].wait()
+
+
+def final(total_size, reduced, wst, pst):
     terms, _, rows = wst.shape
-    cols = factor_inverse.shape[0]
-    whole = pl.BlockSpec(memory_space=pltpu.VMEM)
-    per_term = lambda a: pl.BlockSpec((1,) + a.shape[1:], lambda t: (t, 0, 0))
+    cols, n_prev = wst.shape[1] // 2, pst.shape[1] // 2
+    vmem = pl.BlockSpec(memory_space=pltpu.VMEM)
+    hbm = pl.BlockSpec(memory_space=pl.ANY)
+    small = jax.ShapeDtypeStruct((n_prev, cols), F32)
+    dma = pltpu.SemaphoreType.DMA
     return pl.pallas_call(
-        final_kernel,
-        grid=(terms,),
-        out_shape=jax.ShapeDtypeStruct((terms, cols, rows), BF),
-        in_specs=[whole] * 2 + [per_term(wst), per_term(pst)],
-        out_specs=pl.BlockSpec((1, cols, rows), lambda t: (t, 0, 0)),
-    )(factor_inverse, mix, wst, pst)
-
-
-exact_mode = lax.Precision.HIGHEST
-
-
-def exact(a, b):
-    return jnp.dot(a, b, precision=exact_mode)
+        functools.partial(final_kernel, total_size),
+        out_shape=(jax.ShapeDtypeStruct((terms, cols, rows), BF), small, small, jax.ShapeDtypeStruct((cols, cols), F32)),
+        in_specs=[vmem, hbm, hbm],
+        out_specs=(hbm, vmem, vmem, vmem),
+        scratch_shapes=[
+            pltpu.VMEM((terms, 2 * cols + 2 * n_prev, rows), BF),
+            pltpu.VMEM((terms, cols, rows), BF),
+            dma((2, terms)), dma((terms,)),
+        ],
+        compiler_params=pltpu.CompilerParams(vmem_limit_bytes=40 * 1024 * 1024),
+    )(reduced, wst, pst)
 
 
 def body(n_blk, n_col, blocks, offsets, krylov, previous, node_table, node_index, pole_values, scaling):
     terms, cols, rows = krylov.shape
-    n_prev = previous.shape[0]
-    wst, pst, sums, last, basis = expand(
+    wst, pst, reduced = expand(
         n_blk, n_col, blocks, offsets, krylov, previous, node_table, node_index, pole_values, scaling)
-    total_size = rows * n_blk * terms * n_col
-    inverse_size = 1.0 / total_size
-    root_size = math.sqrt(total_size)
-    local_cross = (sums[:n_prev] + sums[n_prev:2 * n_prev] + last) * inverse_size
-    low = sums[2 * n_prev + cols:]
-    local_self = (sums[2 * n_prev:2 * n_prev + cols] + low + low.T) * inverse_size
-    low = basis[n_prev:]
-    local_basis = (basis[:n_prev] + low + low.T) * inverse_size
-    cross, basis_gram, self_gram = lax.psum((local_cross, local_basis, local_self), ("blk", "col"))
-    coeff_two = cross - exact(basis_gram, cross)
-    combined = cross + coeff_two
-    mixed = exact(combined.T, cross)
-    gram = self_gram - mixed - mixed.T + exact(combined.T, exact(basis_gram, combined))
-    factor = jnp.linalg.cholesky(gram)
-    identity = jnp.eye(cols, dtype=F32)
-    inverse_factor = jax.scipy.linalg.solve_triangular(factor, identity, lower=True)
-    new_basis = final(inverse_factor, -exact(inverse_factor, combined.T), wst, pst)
-    return (new_basis, cross * root_size, coeff_two * root_size, factor)
+    return final(rows * n_blk * terms * n_col, reduced, wst, pst)
 
 
 def solution(mesh):

time: 151 us -> 106 us (0.70)
  blocking collectives: 39.4 us -> 0 us
  other arithmetic: 15.1 us -> 0 us
  Pallas kernels: 89.3 us -> 99.6 us
  matrix products: 1.84 us -> 0 us
  local copies, waits for them, and re-layouts: 3.51 us -> 5.21 us
    psum x1 -> x0, blocking collectives: 39.4 us -> none  [body(): lax.psum((local_cross, local_basis, local_self), ('blk', 'col'))]
    another operation x5 -> x0, other arithmetic: 12.7 us -> none  [the longest x3 6.52 us: body(): factor = jnp.linalg.cholesky(gram)]
    pallas_call x1, Pallas kernels: 80.7 us -> 88.4 us  [expand(): pl.pallas_call(functools.partial(expand_kernel, n_blk, n_col, terms, cols...]
    unnamed x4 -> x6, local copies, waits for them, and re-layouts: 1.4 us -> 5.21 us
    pallas_call x1, Pallas kernels: 8.6 us -> 11.2 us  [final(): pl.pallas_call(functools.partial(final_kernel, total_size), out_shape=(ja...]
    pallas_call x2 -> x0, local copies, waits for them, and re-layouts: 1.81 us -> none  [expand(): pl.pallas_call(functools.partial(expand_kernel, n_blk, n_col, terms, cols...]
    dot_general x5 -> x0, matrix products: 1.61 us -> none  [exact(): return jnp.dot(a, b, precision=exact_mode)]
    add x2 -> x0, other arithmetic: 1.58 us -> none  [the longest x1 0.79 us: body(): local_basis = (basis[:n_prev] + low + low.T) * inverse_size]
where the time goes in v1:
time: 106 us
  Pallas kernels  99.6 us (94%)
  local copies, waits for them, and re-layouts  5.21 us (5%)
    pallas_call x1, Pallas kernels, expand(): pl.pallas_call(functools.partial(expand_kernel, n_blk, n_col, terms, cols...  88.4 us
    pallas_call x1, Pallas kernels, final(): pl.pallas_call(functools.partial(final_kernel, total_size), out_shape=(ja...  11.2 us
    unnamed x6, local copies, waits for them, and re-layouts  5.21 us

profile of v1, /device:TPU:0, one launch (start us, length us, event | category | flops | bytes accessed | tf_op | source)
XLA Modules:
  0.0 105.6 jit_solution(7205729484165768773)
XLA Ops:
  0.6 88.4 %shard_map.111 = (bf16[8,128,2048]{2,1,0:T(8,128)(2,1)}, bf16[8,128,2048]{2,1,0:T(8,128)(2,1)}, f32[128,128]{1,0:T(8,128)}) custom-call(s32[1,2]{1,0:T(1,128)} %offsets.1, s32[8]{0:T(128)} %node_index.1, f32[32]{0:T(128)} %node_table.1, f32[8]{0:T(128)} %pole_values.1, f32[8]{0:T(128)} %scaling.1, bf16[8,64,2048]{2,1,0:T(8,128)(2,1)} %krylov.1, ...), custom_call_target="tpu_custom_call" | custom-call | tf_op jit(solution)/shard_map/pallas_call | solution.py:289
  89.1 0.0 copy-start
  89.1 2.2 %copy-done = bf16[8,128,2048]{2,1,0:T(8,128)(2,1)S(1)} copy-done((bf16[8,128,2048]{2,1,0:T(8,128)(2,1)S(1)}, bf16[8,128,2048]{2,1,0:T(8,128)(2,1)}, u32[]{:S(2)}) %copy-start) | copy-done | bytes 4194328
  91.3 0.0 copy-start.1
  91.3 2.2 %copy-done.1 = bf16[8,128,2048]{2,1,0:T(8,128)(2,1)S(1)} copy-done((bf16[8,128,2048]{2,1,0:T(8,128)(2,1)S(1)}, bf16[8,128,2048]{2,1,0:T(8,128)(2,1)}, u32[]{:S(2)}) %copy-start.1) | copy-done | bytes 4194328
  93.4 0.0 copy-start.2
  93.4 0.8 copy-done.2
  94.3 11.2 %shard_map.112 = (bf16[8,64,2048]{2,1,0:T(8,128)(2,1)}, f32[64,64]{1,0:T(8,128)}, f32[64,64]{1,0:T(8,128)}, f32[64,64]{1,0:T(8,128)}) custom-call(f32[128,128]{1,0:T(8,128)S(1)} %copy-done.2, bf16[8,128,2048]{2,1,0:T(8,128)(2,1)S(1)} %copy-done, bf16[8,128,2048]{2,1,0:T(8,128)(2,1)S(1)} %copy-done.1), custom_call_target="tpu_custom_call" | custom-call | tf_op jit(solution)/shard_map/pallas_call | solution.py:387
Async XLA Ops:
  89.1 2.2 %copy-start = (bf16[8,128,2048]{2,1,0:T(8,128)(2,1)S(1)}, bf16[8,128,2048]{2,1,0:T(8,128)(2,1)}, u32[]{:S(2)}) copy-start(bf16[8,128,2048]{2,1,0:T(8,128)(2,1)} %get-tuple-element.8.w_in) | copy-start | bytes 12582916
  91.3 2.2 %copy-start.1 = (bf16[8,128,2048]{2,1,0:T(8,128)(2,1)S(1)}, bf16[8,128,2048]{2,1,0:T(8,128)(2,1)}, u32[]{:S(2)}) copy-start(bf16[8,128,2048]{2,1,0:T(8,128)(2,1)} %get-tuple-element.9.p_in) | copy-start | bytes 12582916
  93.4 0.8 copy-start.2

commit v2 on v1

--- a/solution.py
+++ b/solution.py
@@ -191,15 +191,17 @@
         plan.setdefault(j // 2, []).append(functools.partial(arrange, j))
     for t in range(terms):
         plan.setdefault(-(-n_prev // 32) + t // 3, []).append(functools.partial(basis_term, t))
-    first = groups[0]
+    first, second, third = groups
     begin = min(terms - 1, first[-1] + 2)
-    plan.setdefault(begin, []).append(functools.partial(ready, first))
-    left = terms - begin
-    chunk = -(-n_tiles // left)
-    for j in range(left):
-        count = min(chunk, n_tiles - j * chunk)
-        if count > 0:
-            plan.setdefault(begin + j, []).append(functools.partial(image_part, first, j * chunk, count))
+    half = n_tiles // 2
+    plan.setdefault(begin, []).extend([
+        functools.partial(ready, first), functools.partial(image_part, first, 0, half)])
+    plan.setdefault(begin + 1, []).append(functools.partial(image_part, first, half, n_tiles - half))
+    plan.setdefault(begin + 2, []).extend([
+        functools.partial(finish, first), functools.partial(ready, second),
+        functools.partial(image_part, second, 0, half)])
+    plan.setdefault(begin + 3, []).extend([
+        functools.partial(image_part, second, half, n_tiles - half), functools.partial(finish, second)])
 
     for k in range(terms + 1):
         if k < terms:
@@ -217,11 +219,9 @@
                 d_copy[k - 1].start()
         for item in plan.get(k, ()):
             item()
-    finish(first)
-    for group in groups[1:]:
-        ready(group)
-        image_part(group, 0, n_tiles)
-        finish(group)
+    ready(third)
+    image_part(third, 0, n_tiles)
+    finish(third)
     low = sums[2 * n_prev + cols:]
     head = jnp.concatenate([
         sums[:n_prev] + sums[n_prev:2 * n_prev] + last_sum[...],
@@ -394,7 +394,7 @@
             pltpu.VMEM((terms, cols, rows), BF),
             dma((2, terms)), dma((terms,)),
         ],
-        compiler_params=pltpu.CompilerParams(vmem_limit_bytes=40 * 1024 * 1024),
+        compiler_params=pltpu.CompilerParams(vmem_limit_bytes=60 * 1024 * 1024),
     )(reduced, wst, pst)
 
 

time: 106 us -> 95.6 us (0.902)
  local copies, waits for them, and re-layouts: 5.21 us -> 0 us
  Pallas kernels: 99.6 us -> 94.7 us
    unnamed x6 -> x0, local copies, waits for them, and re-layouts: 5.21 us -> none
    pallas_call x1, Pallas kernels: 88.4 us -> 83.4 us  [expand(): pl.pallas_call(functools.partial(expand_kernel, n_blk, n_col, terms, cols...]
where the time goes in v2:
time: 95.6 us; the launch traced here: 95.4 us
  Pallas kernels  94.7 us (99%)
    pallas_call x1, Pallas kernels, expand(): pl.pallas_call(functools.partial(expand_kernel, n_blk, n_col, terms, cols...  83.4 us
    pallas_call x1, Pallas kernels, final(): pl.pallas_call(functools.partial(final_kernel, total_size), out_shape=(ja...  11.3 us

profile of v2, /device:TPU:0, one launch (start us, length us, event | category | flops | bytes accessed | tf_op | source)
XLA Modules:
  0.0 95.4 jit_solution(4892078748462173302)
XLA Ops:
  0.6 83.4 %shard_map.111 = (bf16[8,128,2048]{2,1,0:T(8,128)(2,1)}, bf16[8,128,2048]{2,1,0:T(8,128)(2,1)}, f32[128,128]{1,0:T(8,128)}) custom-call(s32[1,2]{1,0:T(1,128)} %offsets.1, s32[8]{0:T(128)} %node_index.1, f32[32]{0:T(128)} %node_table.1, f32[8]{0:T(128)} %pole_values.1, f32[8]{0:T(128)} %scaling.1, bf16[8,64,2048]{2,1,0:T(8,128)(2,1)} %krylov.1, ...), custom_call_target="tpu_custom_call" | custom-call | tf_op jit(solution)/shard_map/pallas_call | solution.py:289
  84.1 11.3 %shard_map.112 = (bf16[8,64,2048]{2,1,0:T(8,128)(2,1)}, f32[64,64]{1,0:T(8,128)}, f32[64,64]{1,0:T(8,128)}, f32[64,64]{1,0:T(8,128)}) custom-call(f32[128,128]{1,0:T(8,128)} %get-tuple-element.7.reduced, bf16[8,128,2048]{2,1,0:T(8,128)(2,1)} %get-tuple-element.8.w_in, bf16[8,128,2048]{2,1,0:T(8,128)(2,1)} %get-tuple-element.9.p_in), custom_call_target="tpu_custom_call" | custom-call | tf_op jit(solution)/shard_map/pallas_call | solution.py:387
